TPU v7x, 128 devices: a whole 4x4x4 slice. The times are simulated.
128 devices in a mesh: seq: 32 (over y, x, core), tp: 4 (over z).
Axes of the slice: x: 4, y: 4, z: 4, core: 2. Of those that a mesh axis runs over, the one named last changes fastest.
Arguments:
- hidden: bfloat16 [32768, 2560], P('seq', 'tp'), may hold values from -6 to 6
- gate_proj: bfloat16 [2560, 5120], P(None, 'tp'), may hold values from -0.125 to 0.125
- input_proj: bfloat16 [2560, 5120], P(None, 'tp'), may hold values from -0.125 to 0.125
- bc_proj: bfloat16 [2560, 256], replicated, may hold values from -0.125 to 0.125
- step_proj: bfloat16 [2560, 80], P(None, 'tp'), may hold values from -0.125 to 0.125
- step_bias: float32 [80], P('tp'), may hold values from -16 to -3
- decay_log: float32 [80], P('tp'), may hold values from 0 to 2.78
- conv_weight: float32 [4, 5120], P(None, 'tp'), may hold values from -3 to 3
- conv_bias: float32 [5120], P('tp'), may hold values from -3 to 3
- bc_conv_weight: float32 [4, 256], replicated, may hold values from -3 to 3
- bc_conv_bias: float32 [256], replicated, may hold values from -3 to 3
- skip_gain: float32 [80], P('tp'), may hold values from 0.5 to 2
- norm_gain: float32 [5120], P('tp'), may hold values from 0.1 to 1.9
- out_proj: bfloat16 [5120, 2560], P('tp'), may hold values from -0.078125 to 0.078125
- amax_history: float32 [16], replicated, may hold values from 1.5 to 4
Outputs:
- mixed: bfloat16 [32768, 2560], P('seq', 'tp')
- new_history: float32 [16], replicated
All inputs are finite; a program needn't handle non-finite values.
Results may differ from a plain program's by a relative error of at most 0.015.
Values may be sent and summed in bfloat16 or wider, within the bound.
A program may use at most 192 MiB of HBM per device.

v0:
```python
import jax
import jax.numpy as jnp
from jax import lax
from jax.sharding import Mesh
from jax.sharding import PartitionSpec as P

BLOCK = 256
INNER = 5120
SEQ = ("seq_0", "seq_1", "seq_2")
QMAX = 448.0
EPS = 1e-05


def shifted(x, axis, by):
    size = lax.axis_size(axis)
    pairs = [(i, i + by) for i in range(size) if 0 <= i + by < size]
    return lax.ppermute(x, axis, pairs)


def nothing_yet(x, identity):
    return jax.tree.map(
        lambda part, zero: jnp.zeros_like(part) + jnp.asarray(zero, part.dtype), x, identity
    )


def entering(x, axes, combine, identity):
    before = start = nothing_yet(x, identity)
    subtotal = x
    for axis in reversed(axes):
        size, here = (lax.axis_size(axis), lax.axis_index(axis))
        pieces = jax.tree.map(
            lambda part, kind: lax.all_gather(part.astype(kind), axis),
            subtotal,
            (jnp.bfloat16, jnp.bfloat16),
        )
        inside, subtotal = (start, start)
        for k in range(size):
            passed = k < here
            subtotal = combine(
                subtotal, jax.tree.map(lambda part, own: part[k].astype(own.dtype), pieces, x)
            )
            inside = jax.tree.map(lambda new, old: jnp.where(passed, new, old), subtotal, inside)
        before = combine(inside, before)
    return before


def from_everyone(x, axis):
    size = lax.axis_size(axis)
    return lax.all_to_all(jnp.broadcast_to(x[None], (size, *x.shape)), axis, 0, 0, tiled=True)


def gathered_once(x, axis):
    leaves = jax.tree.leaves(x)
    turns = sorted(range(len(leaves)), key=lambda k: -leaves[k].size)
    width = (1, *leaves[turns[0]].shape)[-1]
    lines = [
        jnp.pad(leaves[k].reshape(-1), (0, -leaves[k].size % width)).reshape(-1, width)
        for k in turns
    ]
    both, at, found = (from_everyone(jnp.concatenate(lines), axis), 0, {})
    for k, line in zip(turns, lines):
        section = both[:, at : at + len(line)].reshape(len(both), -1)
        found[k] = section[:, : leaves[k].size].reshape(-1, *leaves[k].shape)
        at += len(line)
    numbers = iter(range(len(leaves)))
    return jax.tree.map(lambda _: found[next(numbers)], x)


def collected_alike(x, axis):
    leaves, found = (jax.tree.leaves(x), {})
    for first, a in enumerate(leaves):
        if first not in found:
            alike = [k for k, b in enumerate(leaves) if b.dtype == a.dtype]
            got = (
                gathered_once([leaves[k] for k in alike], axis)
                if len(alike) > 1
                else [from_everyone(a, axis)]
            )
            for k, b in zip(alike, got):
                found[k] = b
    numbers = iter(range(len(leaves)))
    return jax.tree.map(lambda _: found[next(numbers)], x)


def combined_pairwise(pieces, combine):
    while len(jax.tree.leaves(pieces)[0]) > 1:
        pieces = jax.vmap(combine)(
            *(jax.tree.map(lambda part: part[side::2], pieces) for side in (0, 1))
        )
    return jax.tree.map(lambda part: part[0], pieces)


def combined_all(x, axis, combine):
    pieces = collected_alike(x, axis)
    return combined_pairwise(pieces, combine)


def of_everyone(x, axis):
    everything = from_everyone(x, axis)
    return jnp.max(everything, axis=0)


def conv_silu(pre_conv, rim_rows, weight, conv_shift):
    row_count = pre_conv.shape[0]
    kernel = weight.shape[0]
    padded = jnp.concatenate([rim_rows, pre_conv], axis=0)
    running = jnp.zeros(pre_conv.shape, jnp.float32)
    for offset in range(kernel):
        running = running + weight[offset] * padded[offset : offset + row_count].astype(jnp.float32)
    return jax.nn.silu(running + conv_shift).astype(jnp.bfloat16)


def ssd_block(carry_state, block_data):
    x_block, b_block, c_block, step_block, decay_block = block_data
    length = x_block.shape[0]
    head_count = carry_state.shape[0]
    head_width = carry_state.shape[1]
    cum_decay = jnp.cumsum(decay_block, axis=1)
    scores = jnp.dot(c_block, b_block.T, preferred_element_type=jnp.float32)
    causal = lax.broadcasted_iota(jnp.int32, (length, length), 0) >= lax.broadcasted_iota(
        jnp.int32, (length, length), 1
    )
    decay_gap = cum_decay[:, :, None] - cum_decay[:, None, :]
    decay_mask = jnp.where(causal, jnp.exp(jnp.where(causal, decay_gap, 0.0)), 0.0)
    weights = (scores[None] * decay_mask * step_block[:, None, :]).astype(jnp.bfloat16)
    x_heads = x_block.reshape(length, head_count, head_width)
    intra_out = jnp.einsum("hts,shp->htp", weights, x_heads, preferred_element_type=jnp.float32)
    inter_out = jnp.exp(cum_decay)[:, :, None] * jnp.einsum(
        "tn,hpn->htp", c_block.astype(jnp.float32), carry_state
    )
    tail_decay = jnp.exp(cum_decay[:, -1:] - cum_decay) * step_block
    x_weighted = (tail_decay.T[:, :, None] * x_heads.astype(jnp.float32)).astype(jnp.bfloat16)
    update = jnp.einsum("shp,sn->hpn", x_weighted, b_block, preferred_element_type=jnp.float32)
    next_state = jnp.exp(cum_decay[:, -1])[:, None, None] * carry_state + update
    block_out = (intra_out + inter_out).transpose(1, 0, 2).reshape(length, head_count * head_width)
    return (next_state, block_out)


def chain(earlier, later):
    return (earlier[0] + later[0], jnp.exp(later[0])[..., None, None] * earlier[1] + later[1])


def joint(first, second):
    return (first[0] + second[0], jnp.maximum(first[1], second[1]))


def shards(
    hidden,
    gate_proj,
    input_proj,
    bc_proj,
    step_proj,
    step_bias,
    decay_log,
    conv_weight,
    conv_bias,
    bc_conv_weight,
    bc_conv_bias,
    skip_gain,
    norm_gain,
    out_proj,
    amax_history,
):
    row_count = hidden.shape[0]
    inner_local = gate_proj.shape[1]
    state_width = bc_proj.shape[1] // 2
    head_count = step_proj.shape[1]
    head_width = inner_local // head_count
    kernel = conv_weight.shape[0]
    matrices = (gate_proj, input_proj, bc_proj, step_proj)
    piece = lax.all_gather(hidden, "tp", axis=1, tiled=True)
    gate_raw, x_raw, bc_raw, step_raw = tuple(
        (jnp.dot(piece, matrix, preferred_element_type=jnp.float32) for matrix in matrices)
    )
    gate_in = gate_raw.astype(jnp.bfloat16)
    x_pre = x_raw.astype(jnp.bfloat16)
    bc_pre = bc_raw.astype(jnp.bfloat16)
    x_rim, bc_rim = shifted(
        (x_pre[row_count - kernel + 1 :], bc_pre[row_count - kernel + 1 :]), SEQ, 1
    )
    x_conv = conv_silu(x_pre, x_rim, conv_weight, conv_bias)
    bc_conv = conv_silu(bc_pre, bc_rim, bc_conv_weight, bc_conv_bias)
    b_in = bc_conv[:, :state_width]
    c_out = bc_conv[:, state_width:]
    step_size = jax.nn.softplus(step_raw + step_bias)
    log_decay = step_size * -jnp.exp(decay_log)
    blocks = row_count // BLOCK
    stacked = (
        x_conv.reshape(blocks, BLOCK, inner_local),
        b_in.reshape(blocks, BLOCK, state_width),
        c_out.reshape(blocks, BLOCK, state_width),
        step_size.reshape(blocks, BLOCK, head_count).transpose(0, 2, 1),
        log_decay.reshape(blocks, BLOCK, head_count).transpose(0, 2, 1),
    )
    zero_state = jnp.zeros((head_count, head_width, state_width), jnp.float32)
    local_state, block_outs = lax.scan(ssd_block, zero_state, stacked)
    total_decay = jnp.sum(log_decay, axis=0)
    entry_decay, incoming = entering(
        (total_decay, local_state), SEQ, chain, (jnp.zeros_like(total_decay), zero_state)
    )
    reach = jnp.exp(jnp.cumsum(log_decay, axis=0))
    carried = jnp.einsum("tn,hpn->thp", c_out.astype(jnp.float32), incoming)
    ssm_out = block_outs.reshape(row_count, inner_local) + (reach[:, :, None] * carried).reshape(
        row_count, inner_local
    )
    x_heads = x_conv.reshape(row_count, head_count, head_width).astype(jnp.float32)
    ssm_out = ssm_out + (skip_gain[:, None] * x_heads).reshape(row_count, inner_local)
    gated = ssm_out * jax.nn.silu(gate_in.astype(jnp.float32))
    local_squares = jnp.sum(gated * gated, axis=1)
    row_peak = jnp.max(jnp.abs(gated * norm_gain), axis=1)
    squares, row_top = combined_all((local_squares, row_peak), "tp", joint)
    inv_rms = lax.rsqrt(squares / INNER + EPS)
    normed = gated * inv_rms[:, None] * norm_gain
    peak_value = of_everyone(jnp.max(row_top * inv_rms), SEQ)
    scale = QMAX / jnp.max(amax_history)
    quant = jnp.clip(normed * scale, -QMAX, QMAX).astype(jnp.bfloat16)
    partial_value = jnp.dot(quant, out_proj, preferred_element_type=jnp.float32)
    summed = lax.psum_scatter(
        partial_value.astype(jnp.bfloat16), "tp", scatter_dimension=1, tiled=True
    ).astype(jnp.float32)
    mixed = (summed / scale).astype(jnp.bfloat16)
    new_history = jnp.concatenate([jnp.reshape(peak_value, (1,)), amax_history[:-1]])
    return (mixed, new_history)


def solution(mesh):
    finer = Mesh(mesh.devices.reshape(4, 4, 2, mesh.shape["tp"]), ("seq_0", "seq_1", "seq_2", "tp"))
    in_specs = (
        P(SEQ, "tp"),
        P(None, "tp"),
        P(None, "tp"),
        P(),
        P(None, "tp"),
        P("tp"),
        P("tp"),
        P(None, "tp"),
        P("tp"),
        P(),
        P(),
        P("tp"),
        P("tp"),
        P("tp", None),
        P(),
    )
    out_specs = (P(SEQ, "tp"), P())
    return jax.shard_map(
        shards, mesh=finer, in_specs=in_specs, out_specs=out_specs, check_vma=False
    )
```

profile of v0, /device:TPU:1, one launch (start us, length us, event | category | flops | bytes accessed | tf_op | source)
XLA Modules:
  0.0 332.2 jit_solution(15634064660990956811)
XLA Ops:
  12.3 57.5 %all-gather.8.cloned.1.call-done = bf16[1024,2560]{1,0:T(8,128)(2,1)} async-done(((bf16[1024,640]{1,0:T(8,128)(2,1)}), bf16[1024,2560]{1,0:T(8,128)(2,1)}) %all-gather.8.cloned.1.call-update) | async-done | bytes 5242896 | tf_op jit(solution)/shard_map/all_gather | solution.py:171
  69.9 4.1 %convolution_convert_fusion.3 = bf16[1024,256]{1,0:T(8,128)(2,1)S(1)} fusion(bf16[1024,2560]{1,0:T(8,128)(2,1)} %all-gather.8.cloned.1.call-done, bf16[2560,256]{1,0:T(8,128)(2,1)S(1)} %copy-done), kind=kOutput, calls=%fused_computation.68 | convolution fusion | flops 1342439424 | bytes 7077888 | tf_op jit(solution)/shard_map/dot_general | solution.py:173
  74.1 4.0 %collective-permute-start.1 = (bf16[3,256]{1,0:T(4,128)(2,1)S(1)}, bf16[3,256]{1,0:T(4,128)(2,1)S(1)}, u32[]{:S(2)}, u32[]{:S(2)}) collective-permute-start(bf16[3,256]{1,0:T(4,128)(2,1)S(1)} %slice.240), channel_id=1, source_target_pairs={{0,4},{4,8},{8,12},{12,16},{16,20},{20,24},{24,28},{28,32},{32,36}... | collective-permute-start | bytes 4616 | tf_op jit(solution)/shard_map/ppermute | solution.py:17
  78.1 10.0 %convolution_convert_fusion.2 = bf16[1024,1280]{1,0:T(8,128)(2,1)S(1)} fusion(bf16[1024,2560]{1,0:T(8,128)(2,1)S(1)} %copy-done.3, bf16[2560,1280]{1,0:T(8,128)(2,1)} %param.19), kind=kOutput, calls=%fused_computation.55 | convolution fusion | flops 6712197120 | bytes 14417920 | tf_op jit(solution)/shard_map/dot_general | solution.py:173
  88.1 2.1 collective-permute-start
  90.2 2.2 fusion.111
  92.9 2.6 all-reduce
  97.6 8.2 %multiply_convert_fusion.4 = bf16[1024,1280]{1,0:T(8,128)(2,1)} fusion(bf16[1024,1280]{1,0:T(8,128)(2,1)} %copy-done.6, bf16[3,1280]{1,0:T(4,128)(2,1)S(1)} %collective-permute-done, f32[1280]{0:T(1024)S(1)} %copy-done.11, f32[1280]{0:T(1024)S(1)} %get-tuple-element.126, f32[1280]{0:T(1024)S(1)} %get-tuple-element.127, f32[1280]{0:T(1024)S(1)} %get-tuple-element.125, ...), kind=kLoop, calls=%fused_computation.53 | loop fusion | flops 34078720 | bytes 5276160 | tf_op jit(solution)/shard_map/convert_element_type | solution.py:110
  105.9 47.1 %while.13 = (s32[]{:T(128)}, f32[20,64,128]{2,1,0:T(8,128)S(1)}, f32[4,256,1280]{2,1,0:T(8,128)}, f32[4,20,256]{2,1,0:T(8,128)}, f32[4,20,256]{2,1,0:T(8,128)}, ...) while((s32[]{:T(128)}, f32[20,64,128]{2,1,0:T(8,128)S(1)}, ...), condition=%wide.region_3.4_spmd.clone, body=%wide.region_0.3_spmd.clone.sunk | while | flops 363210816 | bytes 22548344 | solution.py:196
  107.8 1.4 multiply_bitcast_fusion.3
  110.8 1.7 fusion.172
  119.6 1.4 multiply_bitcast_fusion.3
  122.6 1.7 fusion.172
  134.4 1.7 fusion.172
  146.2 1.7 fusion.172
  153.1 2.6 all-gather.1
  156.8 7.9 %all-gather.2 = bf16[4,1,20]{2,1,0:T(2,128)(2,1)S(1)} all-gather(bf16[1,1,20]{2,1,0:T(2,128)(2,1)} %get-tuple-element.170), channel_id=1, replica_groups=mesh['seq_0'=4,'seq_1'=4,'seq_2'=2,'tp'=4] {'seq_1'}, dimensions={0}, use_global_device_ids=true | all-gather | bytes 200 | tf_op jit(solution)/shard_map/all_gather | solution.py:32
  164.8 15.5 %all-gather.10.cloned.1.call-done = bf16[4,20,64,128]{3,2,1,0:T(8,128)(2,1)} async-done(((bf16[1,20,64,128]{3,2,1,0:T(8,128)(2,1)}), bf16[4,20,64,128]{3,2,1,0:T(8,128)(2,1)}) %all-gather.10.cloned.1.call-update) | async-done | bytes 1310736 | tf_op jit(solution)/shard_map/all_gather | solution.py:32
  180.3 2.4 fusion.60
  182.9 5.6 %reduce-window.16 = f32[20,8,128]{2,1,0:T(8,128)S(1)} reduce-window(f32[20,8,128]{2,1,0:T(8,128)S(1)} %slice.273, f32[]{:T(128)} %constant.37.clone.1), window={size=1x1x128 pad=0_0x0_0x127_0}, to_apply=%region_4.5 | reduce-window | flops 2600960 | bytes 163844 | tf_op jit(solution)/shard_map/reduce-window.2
  189.0 7.7 %all-gather.3 = bf16[4,1,20]{2,1,0:T(2,128)(2,1)S(1)} all-gather(bf16[1,1,20]{2,1,0:T(2,128)(2,1)S(1)} %get-tuple-element.164), channel_id=1, replica_groups=mesh['seq_0'=4,'seq_1'=4,'seq_2'=2,'tp'=4] {'seq_0'}, dimensions={0}, use_global_device_ids=true | all-gather | bytes 200 | tf_op jit(solution)/shard_map/all_gather | solution.py:32
  196.7 11.5 %all-gather.12.cloned.1.call-done = bf16[4,20,64,128]{3,2,1,0:T(8,128)(2,1)} async-done(((bf16[1,20,64,128]{3,2,1,0:T(8,128)(2,1)}), bf16[4,20,64,128]{3,2,1,0:T(8,128)(2,1)}) %all-gather.12.cloned.1.call-update) | async-done | bytes 1310736 | tf_op jit(solution)/shard_map/all_gather | solution.py:32
  208.3 5.8 %broadcast_multiply_fusion = f32[1024,20,64]{0,2,1:T(8,128)} fusion(f32[1024,20]{0,1:T(8,128)S(1)} %bitcast.302, bf16[4,20,64,128]{3,2,1,0:T(8,128)(2,1)} %all-gather.12.cloned.1.call-done, f32[20]{0:T(128)S(1)} %get-tuple-element.171, f32[20]{0:T(128)S(1)} %get-tuple-element.169, f32[20]{0:T(128)S(1)} %get-tuple-element.168, ...), kind=kOutput, calls=%fused_computation.66 | convolution fusion | flops 343572480 | bytes 8886282 | tf_op jit(solution)/shard_map/tn,hpn->thp/dot_general | solution.py:202
  214.1 5.9 %copy.71 = f32[1024,1280]{1,0:T(8,128)} copy(f32[1024,1280]{0,1:T(8,128)} %bitcast.291) | data formatting | bytes 10485760 | tf_op jit(solution)/shard_map/reshape | solution.py:203
  220.0 16.0 %multiply_reduce_fusion = (f32[1024]{0:T(1024)S(1)}, f32[1024]{0:T(1024)S(1)}, f32[1024,1280]{1,0:T(8,128)}) fusion(f32[1280]{0:T(1024)S(1)} %copy-done.15, bf16[1024,2560]{1,0:T(8,128)(2,1)} %all-gather.8.cloned.1.call-done, bf16[2560,1280]{1,0:T(8,128)(2,1)} %param.18, bf16[1024,1280]{1,0:T(8,128)(2,1)} %bitcast.290, f32[1280]{0:T(1024)S(1)} %mul.413, ...), kind=kOutput, calls=%fused_computation.52 | convolution fusion | flops 6731855872 | bytes 30164992 | tf_op jit(solution)/shard_map/dot_general | solution.py:173
  236.6 4.1 %all-to-all-start = ((f32[4,2,1024]{2,1,0:T(2,128)}), f32[4,2,1024]{2,1,0:T(2,128)S(1)}, u32[]{:S(2)}, u32[]{:S(2)}) async-start(f32[4,2,1024]{2,1,0:T(2,128)} %broadcast_in_dim.33), calls=%async_computation | async-start | bytes 65536 | tf_op jit(solution)/shard_map/all_to_all | solution.py:49
  242.1 3.0 all-to-all-done
  245.2 12.7 %convolution_convert_fusion = bf16[1024,2560]{1,0:T(8,128)(2,1)} fusion(bf16[1280,2560]{1,0:T(8,128)(2,1)} %param.30, f32[1024,1280]{1,0:T(8,128)} %get-tuple-element.174, f32[]{:T(128)S(6)} %div.31, f32[1024]{0:T(1024)S(1)} %bitcast.307, f32[1280]{0:T(1024)S(1)} %copy-done.15), kind=kOutput, calls=%fused_computation.43 | convolution fusion | flops 6720061440 | bytes 17048580 | tf_op jit(solution)/shard_map/dot_general | solution.py:217
  257.9 7.9 %copy.73 = bf16[1024,2560]{0,1:T(8,128)(2,1)} copy(bf16[1024,2560]{1,0:T(8,128)(2,1)} %convolution_convert_fusion) | data formatting | bytes 10485760
  267.3 16.1 %all_to_all.11 = f32[32,1,1]{2,1,0:T(1,128)S(1)} all-to-all(f32[32,1,1]{2,1,0:T(1,128)S(1)} %broadcast_in_dim.34), channel_id=1, replica_groups=mesh['seq_0'=4,'seq_1'=4,'seq_2'=2,'tp'=4] {'seq_0','seq_1','seq_2'}, dimensions={0} | all-to-all | bytes 256 | tf_op jit(solution)/shard_map/all_to_all | solution.py:49
  285.2 37.5 %reduce-scatter.4.cloned.1.call-done = bf16[640,1024]{1,0:T(8,128)(2,1)} async-done(((bf16[2560,1024]{1,0:T(8,128)(2,1)}), bf16[640,1024]{1,0:T(8,128)(2,1)}) %reduce-scatter.4.cloned.1.call-update) | async-done | bytes 1310736
  322.7 1.7 copy.74
  (206 shorter events, 51.9 us)
Async XLA Ops:
  7.2 62.7 %copy-start = (bf16[2560,256]{1,0:T(8,128)(2,1)S(1)}, bf16[2560,256]{1,0:T(8,128)(2,1)}, u32[]{:S(2)}) copy-start(bf16[2560,256]{1,0:T(8,128)(2,1)} %param.20) | copy-start | bytes 3932164
  7.2 62.7 %all-gather.8.cloned.1.call-start = ((), (), s32[]{:S(2)}) async-start(), calls=%async_computation.3 | async-start | bytes 6553600 | tf_op jit(solution)/shard_map/all_gather | solution.py:171
  7.9 172.3 %all-gather.10.cloned.1.call-start = ((), (), s32[]{:S(2)}) async-start(), calls=%async_computation.4 | async-start | bytes 1638400 | tf_op jit(solution)/shard_map/all_gather | solution.py:32
  69.9 8.2 %copy-start.3 = (bf16[1024,2560]{1,0:T(8,128)(2,1)S(1)}, bf16[1024,2560]{1,0:T(8,128)(2,1)}, u32[]{:S(2)}) copy-start(bf16[1024,2560]{1,0:T(8,128)(2,1)} %all-gather.8.cloned.1.call-done) | copy-start | bytes 15728644
  74.1 16.1 %copy-start.10 = (bf16[2560,20]{0,1:T(8,128)(2,1)S(1)}, bf16[2560,20]{0,1:T(8,128)(2,1)}, u32[]{:S(2)}) copy-start(bf16[2560,20]{0,1:T(8,128)(2,1)} %param.21) | copy-start | bytes 307204
  74.1 16.1 %copy-start.12 = (f32[20]{0:T(128)S(1)}, f32[20]{0:T(128)}, u32[]{:S(2)}) copy-start(f32[20]{0:T(128)} %param.22) | copy-start | bytes 244
  74.1 22.7 %collective-permute-start.1 = (bf16[3,256]{1,0:T(4,128)(2,1)S(1)}, bf16[3,256]{1,0:T(4,128)(2,1)S(1)}, u32[]{:S(2)}, u32[]{:S(2)}) collective-permute-start(bf16[3,256]{1,0:T(4,128)(2,1)S(1)} %slice.240), channel_id=1, source_target_pairs={{0,4},{4,8},{8,12},{12,16},{16,20},{20,24},{24,28},{28,32},{32,36}... | collective-permute-start | bytes 4616 | tf_op jit(solution)/shard_map/ppermute | solution.py:17
  88.0 4.3 %copy-start.6 = (bf16[1024,1280]{1,0:T(8,128)(2,1)}, bf16[1024,1280]{1,0:T(8,128)(2,1)S(1)}, u32[]{:S(2)}) copy-start(bf16[1024,1280]{1,0:T(8,128)(2,1)S(1)} %convolution_convert_fusion.2) | copy-start | bytes 7864324
  88.1 8.8 %copy-start.13 = (f32[256]{0:T(256)S(1)}, f32[256]{0:T(256)}, u32[]{:S(2)}) copy-start(f32[256]{0:T(256)} %param.27) | copy-start | bytes 3076
  88.1 9.5 %copy-start.11 = (f32[1280]{0:T(1024)S(1)}, f32[1280]{0:T(1024)}, u32[]{:S(2)}) copy-start(f32[1280]{0:T(1024)} %param.25) | copy-start | bytes 15364
  88.1 9.5 %collective-permute-start = (bf16[3,1280]{1,0:T(4,128)(2,1)S(1)}, bf16[3,1280]{1,0:T(4,128)(2,1)S(1)}, u32[]{:S(2)}, u32[]{:S(2)}) collective-permute-start(bf16[3,1280]{1,0:T(4,128)(2,1)S(1)} %slice.235), channel_id=1, source_target_pairs={{0,4},{4,8},{8,12},{12,16},{16,20},{20,24},{24,28},{28,32},{32,36}... | collective-permute-start | bytes 23048 | tf_op jit(solution)/shard_map/ppermute | solution.py:17
  97.5 8.3 %copy-start.7 = (bf16[1024,256]{1,0:T(8,128)(2,1)}, bf16[1024,256]{1,0:T(8,128)(2,1)S(1)}, u32[]{:S(2)}) copy-start(bf16[1024,256]{1,0:T(8,128)(2,1)S(1)} %multiply_convert_fusion.5) | copy-start | bytes 1572868
  105.9 6.6 %copy-start.4 = (bf16[4,256,128]{2,1,0:T(8,128)(2,1)}, bf16[4,256,128]{2,1,0:T(8,128)(2,1)S(1)}, u32[]{:S(2)}) copy-start(bf16[4,256,128]{2,1,0:T(8,128)(2,1)S(1)} %get-tuple-element.260) | copy-start | bytes 786436 | tf_op jit(solution)/shard_map/while
  110.8 1.7 copy-start.2
  114.0 3.6 %copy-start.5 = (bf16[4,256,128]{2,1,0:T(8,128)(2,1)S(1)}, bf16[4,256,128]{2,1,0:T(8,128)(2,1)}, u32[]{:S(2)}) copy-start(bf16[4,256,128]{2,1,0:T(8,128)(2,1)} %copy-done.4) | copy-start | bytes 786436 | tf_op jit(solution)/shard_map/while
  117.7 6.6 %copy-start.4 = (bf16[4,256,128]{2,1,0:T(8,128)(2,1)}, bf16[4,256,128]{2,1,0:T(8,128)(2,1)S(1)}, u32[]{:S(2)}) copy-start(bf16[4,256,128]{2,1,0:T(8,128)(2,1)S(1)} %get-tuple-element.260) | copy-start | bytes 786436 | tf_op jit(solution)/shard_map/while
  122.6 1.7 copy-start.2
  125.8 3.6 %copy-start.5 = (bf16[4,256,128]{2,1,0:T(8,128)(2,1)S(1)}, bf16[4,256,128]{2,1,0:T(8,128)(2,1)}, u32[]{:S(2)}) copy-start(bf16[4,256,128]{2,1,0:T(8,128)(2,1)} %copy-done.4) | copy-start | bytes 786436 | tf_op jit(solution)/shard_map/while
  129.4 6.6 %copy-start.4 = (bf16[4,256,128]{2,1,0:T(8,128)(2,1)}, bf16[4,256,128]{2,1,0:T(8,128)(2,1)S(1)}, u32[]{:S(2)}) copy-start(bf16[4,256,128]{2,1,0:T(8,128)(2,1)S(1)} %get-tuple-element.260) | copy-start | bytes 786436 | tf_op jit(solution)/shard_map/while
  134.3 1.7 copy-start.2
  137.5 3.7 %copy-start.5 = (bf16[4,256,128]{2,1,0:T(8,128)(2,1)S(1)}, bf16[4,256,128]{2,1,0:T(8,128)(2,1)}, u32[]{:S(2)}) copy-start(bf16[4,256,128]{2,1,0:T(8,128)(2,1)} %copy-done.4) | copy-start | bytes 786436 | tf_op jit(solution)/shard_map/while
  141.3 6.6 %copy-start.4 = (bf16[4,256,128]{2,1,0:T(8,128)(2,1)}, bf16[4,256,128]{2,1,0:T(8,128)(2,1)S(1)}, u32[]{:S(2)}) copy-start(bf16[4,256,128]{2,1,0:T(8,128)(2,1)S(1)} %get-tuple-element.260) | copy-start | bytes 786436 | tf_op jit(solution)/shard_map/while
  149.4 3.6 %copy-start.5 = (bf16[4,256,128]{2,1,0:T(8,128)(2,1)S(1)}, bf16[4,256,128]{2,1,0:T(8,128)(2,1)}, u32[]{:S(2)}) copy-start(bf16[4,256,128]{2,1,0:T(8,128)(2,1)} %copy-done.4) | copy-start | bytes 786436 | tf_op jit(solution)/shard_map/while
  153.0 29.7 %copy-start.14 = (f32[20]{0:T(128)S(1)}, f32[20]{0:T(128)}, u32[]{:S(2)}) copy-start(f32[20]{0:T(128)} %param.28) | copy-start | bytes 244
  153.0 29.8 %copy-start.9 = (f32[20,1024]{1,0:T(8,128)S(1)}, f32[20,1024]{1,0:T(8,128)}, u32[]{:S(2)}) copy-start(f32[20,1024]{1,0:T(8,128)} %get-tuple-element.172) | copy-start | bytes 245764
  153.0 55.2 %copy-start.8 = (bf16[1024,256]{1,0:T(8,128)(2,1)S(1)}, bf16[1024,256]{1,0:T(8,128)(2,1)}, u32[]{:S(2)}) copy-start(bf16[1024,256]{1,0:T(8,128)(2,1)} %copy-done.7) | copy-start | bytes 1572868
  156.7 51.5 %all-gather.12.cloned.1.call-start = ((), (), s32[]{:S(2)}) async-start(), calls=%async_computation.5 | async-start | bytes 1638400 | tf_op jit(solution)/shard_map/all_gather | solution.py:32
  214.1 5.9 %copy-start.15 = (f32[1280]{0:T(1024)S(1)}, f32[1280]{0:T(1024)}, u32[]{:S(2)}) copy-start(f32[1280]{0:T(1024)} %param.29) | copy-start | bytes 15364
  220.0 20.8 %copy-start.16 = (f32[16]{0:T(128)S(1)}, f32[16]{0:T(128)}, u32[]{:S(2)}) copy-start(f32[16]{0:T(128)} %param.31) | copy-start | bytes 196
  236.6 8.4 %all-to-all-start = ((f32[4,2,1024]{2,1,0:T(2,128)}), f32[4,2,1024]{2,1,0:T(2,128)S(1)}, u32[]{:S(2)}, u32[]{:S(2)}) async-start(f32[4,2,1024]{2,1,0:T(2,128)} %broadcast_in_dim.33), calls=%async_computation | async-start | bytes 65536 | tf_op jit(solution)/shard_map/all_to_all | solution.py:49
  240.8 81.9 %reduce-scatter.4.cloned.1.call-start = ((), (), s32[]{:S(2)}) async-start(), calls=%async_computation.6 | async-start | bytes 6553600
  265.9 59.8 %copy-start.1 = (bf16[2560,256]{1,0:T(8,128)(2,1)S(1)}, bf16[2560,256]{1,0:T(8,128)(2,1)}, u32[]{:S(2)}) copy-start(bf16[2560,256]{1,0:T(8,128)(2,1)} %param.20) | copy-start | bytes 3932164
  (1 other events, 1.7 us)
Sparse Core Ops, SparseCore 0:
  9.7 60.1 all-gather.7
  156.8 23.3 all-gather.9
  182.8 25.4 all-gather.11
  266.0 56.6 reduce-scatter.3
where the time goes:
time: 334 us; the launch traced here: 332 us
  waiting for transfers between devices  126 us (38%)
  matrix products  67.3 us (20%)
  local copies, waits for them, and re-layouts  38.3 us (11%)
  other arithmetic  37.7 us (11%)
  blocking collectives  36.9 us (11%)
  between operations  15.5 us (5%)
  starting transfers between devices  10.3 us (3%)
    all_gather x1, waiting for transfers between devices, shards(): piece = lax.all_gather(hidden, 'tp', axis=1, tiled=True)  57.5 us
    unnamed x5, waiting for transfers between devices  38.2 us
    dot_general x4, matrix products, shards(): jnp.dot(piece, matrix, preferred_element_type=jnp.float32)  32.3 us
    all_gather x2, waiting for transfers between devices, entering(): lax.all_gather(part.astype(kind), axis)  27 us
    all_gather x3, blocking collectives, entering(): lax.all_gather(part.astype(kind), axis)  18.2 us
    all_to_all x1, blocking collectives, from_everyone(): lax.all_to_all(jnp.broadcast_to(x[None], (size, *x.shape)), axis, 0, 0, t...  16.1 us
    dot_general x1, matrix products, shards(): partial_value = jnp.dot(quant, out_proj, preferred_element_type=jnp.float32)  12.7 us
    unnamed x38, local copies, waits for them, and re-layouts  11.3 us
  transfers between devices with their start and end apart: 7, of which 5 were waited for; matrix products, arithmetic and copies ran while one was open for 9% of the time, Pallas kernels for 0%

commit v1 on v0

--- a/solution.py
+++ b/solution.py
@@ -9,6 +9,18 @@
 SEQ = ("seq_0", "seq_1", "seq_2")
 QMAX = 448.0
 EPS = 1e-05
+
+
+def _state_slots(z, group_axis):
+    return jnp.concatenate(
+        lax.all_to_all(
+            jnp.stack(lax.axis_size(group_axis) * [z], 0),
+            axis_name=group_axis,
+            split_axis=0,
+            concat_axis=0,
+        ),
+        axis=1,
+    )
 
 
 def shifted(x, axis, by):
@@ -168,7 +180,7 @@
     head_width = inner_local // head_count
     kernel = conv_weight.shape[0]
     matrices = (gate_proj, input_proj, bc_proj, step_proj)
-    piece = lax.all_gather(hidden, "tp", axis=1, tiled=True)
+    piece = _state_slots(hidden, "tp")
     gate_raw, x_raw, bc_raw, step_raw = tuple(
         (jnp.dot(piece, matrix, preferred_element_type=jnp.float32) for matrix in matrices)
     )

time: 334 us -> 347 us (1.039)
  starting transfers between devices: 10.3 us -> 16.7 us
  local copies, waits for them, and re-layouts: 38.3 us -> 42.2 us
    all_to_all x0 -> x1, waiting for transfers between devices: none -> 59.2 us  [_state_slots(): lax.all_to_all(jnp.stack(lax.axis_size(group_axis) * [z], 0), axis_name=g...]
    all_gather x1 -> x0, waiting for transfers between devices: 57.5 us -> none  [shards(): piece = lax.all_gather(hidden, 'tp', axis=1, tiled=True)]
    all_to_all x0 -> x1, starting transfers between devices: none -> 5.99 us  [_state_slots(): lax.all_to_all(jnp.stack(lax.axis_size(group_axis) * [z], 0), axis_name=g...]
    unnamed x38 -> x45, local copies, waits for them, and re-layouts: 11.3 us -> 13.8 us
    unnamed x5 -> x4, waiting for transfers between devices: 38.2 us -> 37.5 us
  transfers between devices with their start and end apart: 7 -> 7, of which waited for: 5 -> 5; matrix products, arithmetic and copies ran while one was open for 9% -> 8% of each run, Pallas kernels for 0% -> 0%
where the time goes in v1:
time: 347 us; the launch traced here: 345 us
  waiting for transfers between devices  125 us (36%)
  matrix products  70.6 us (20%)
  local copies, waits for them, and re-layouts  42.2 us (12%)
  blocking collectives  37.1 us (11%)
  other arithmetic  37 us (11%)
  starting transfers between devices  16.7 us (5%)
  between operations  15.5 us (4%)
    all_to_all x1, waiting for transfers between devices, _state_slots(): lax.all_to_all(jnp.stack(lax.axis_size(group_axis) * [z], 0), axis_name=g...  59.2 us
    unnamed x4, waiting for transfers between devices  37.5 us
    dot_general x4, matrix products, shards(): jnp.dot(piece, matrix, preferred_element_type=jnp.float32)  35.6 us
    all_gather x2, waiting for transfers between devices, entering(): lax.all_gather(part.astype(kind), axis)  25.6 us
    all_gather x3, blocking collectives, entering(): lax.all_gather(part.astype(kind), axis)  18.3 us
    all_to_all x1, blocking collectives, from_everyone(): lax.all_to_all(jnp.broadcast_to(x[None], (size, *x.shape)), axis, 0, 0, t...  16.1 us
    unnamed x45, local copies, waits for them, and re-layouts  13.8 us
    dot_general x1, matrix products, shards(): partial_value = jnp.dot(quant, out_proj, preferred_element_type=jnp.float32)  12.7 us
  transfers between devices with their start and end apart: 7, of which 5 were waited for; matrix products, arithmetic and copies ran while one was open for 8% of the time, Pallas kernels for 0%

profile of v1, /device:TPU:1, one launch (start us, length us, event | category | flops | bytes accessed | tf_op | source)
XLA Modules:
  0.0 345.1 jit_solution(67153863533296586)
XLA Ops:
  7.2 1.7 copy.69
  8.9 3.1 stack.2
  12.0 6.0 %all-to-all-start = ((bf16[4,1024,640]{1,2,0:T(8,128)(2,1)}), bf16[4,1024,640]{1,2,0:T(8,128)(2,1)}, u32[]{:S(2)}, u32[]{:S(2)}) async-start(bf16[4,1024,640]{1,2,0:T(8,128)(2,1)} %stack.2), calls=%async_computation | async-start | bytes 10485760 | tf_op jit(solution)/shard_map/all_to_all | solution.py:16
  19.3 59.2 %all-to-all-done = bf16[4,1024,640]{1,2,0:T(8,128)(2,1)} async-done(((bf16[4,1024,640]{1,2,0:T(8,128)(2,1)}), bf16[4,1024,640]{1,2,0:T(8,128)(2,1)}, u32[]{:S(2)}, u32[]{:S(2)}) %all-to-all-start) | async-done | bytes 5242912 | tf_op jit(solution)/shard_map/all_to_all | solution.py:16
  78.5 4.1 %convolution_convert_fusion.3 = bf16[1024,256]{1,0:T(8,128)(2,1)S(1)} fusion(bf16[1024,2560]{0,1:T(8,128)(2,1)} %bitcast.1, bf16[2560,256]{1,0:T(8,128)(2,1)S(1)} %copy-done), kind=kOutput, calls=%fused_computation.68 | convolution fusion | flops 1342439424 | bytes 7077888 | tf_op jit(solution)/shard_map/dot_general | solution.py:185
  82.6 4.5 %collective-permute-start.1 = (bf16[3,256]{1,0:T(4,128)(2,1)S(1)}, bf16[3,256]{1,0:T(4,128)(2,1)S(1)}, u32[]{:S(2)}, u32[]{:S(2)}) collective-permute-start(bf16[3,256]{1,0:T(4,128)(2,1)S(1)} %slice.240), channel_id=1, source_target_pairs={{0,4},{4,8},{8,12},{12,16},{16,20},{20,24},{24,28},{28,32},{32,36}... | collective-permute-start | bytes 4616 | tf_op jit(solution)/shard_map/ppermute | solution.py:29
  87.1 10.9 %convolution_convert_fusion.2 = bf16[1024,1280]{1,0:T(8,128)(2,1)S(1)} fusion(bf16[1024,2560]{0,1:T(8,128)(2,1)} %bitcast.1, bf16[2560,1280]{1,0:T(8,128)(2,1)} %param.19), kind=kOutput, calls=%fused_computation.55 | convolution fusion | flops 6712197120 | bytes 14417920 | tf_op jit(solution)/shard_map/dot_general | solution.py:185
  99.6 2.1 collective-permute-start
  101.6 4.0 %fusion.111 = (f32[20,1024]{1,0:T(8,128)}, f32[1024,20]{0,1:T(8,128)S(1)}) fusion(f32[20]{0:T(128)S(1)} %exponential_negate_fusion, f32[20]{0:T(128)S(1)} %copy-done.12, bf16[1024,2560]{0,1:T(8,128)(2,1)} %bitcast.1, bf16[2560,20]{0,1:T(8,128)(2,1)S(1)} %copy-done.9), kind=kOutput, calls=%fused_computation.161 | convolution fusion | flops 105021440 | bytes 5509280 | tf_op jit(solution)/shard_map/dot_general | solution.py:185
  106.1 2.8 all-reduce
  111.1 8.2 %multiply_convert_fusion.4 = bf16[1024,1280]{1,0:T(8,128)(2,1)} fusion(bf16[1024,1280]{1,0:T(8,128)(2,1)} %copy-done.5, bf16[3,1280]{1,0:T(4,128)(2,1)S(1)} %collective-permute-done, f32[1280]{0:T(1024)S(1)} %copy-done.11, f32[1280]{0:T(1024)S(1)} %get-tuple-element.126, f32[1280]{0:T(1024)S(1)} %get-tuple-element.127, f32[1280]{0:T(1024)S(1)} %get-tuple-element.125, ...), kind=kLoop, calls=%fused_computation.53 | loop fusion | flops 34078720 | bytes 5276160 | tf_op jit(solution)/shard_map/convert_element_type | solution.py:122
  119.3 47.1 %while.13 = (s32[]{:T(128)}, f32[20,64,128]{2,1,0:T(8,128)S(1)}, f32[4,256,1280]{2,1,0:T(8,128)}, f32[4,20,256]{2,1,0:T(8,128)}, f32[4,20,256]{2,1,0:T(8,128)}, ...) while((s32[]{:T(128)}, f32[20,64,128]{2,1,0:T(8,128)S(1)}, ...), condition=%wide.region_3.4_spmd.clone, body=%wide.region_0.3_spmd.clone.sunk | while | flops 363210816 | bytes 22548344 | solution.py:208
  124.3 1.7 fusion.172
  136.1 1.7 fusion.172
  147.8 1.7 fusion.172
  166.5 2.4 all-gather.1
  170.1 8.0 %all-gather.2 = bf16[4,1,20]{2,1,0:T(2,128)(2,1)S(1)} all-gather(bf16[1,1,20]{2,1,0:T(2,128)(2,1)} %get-tuple-element.170), channel_id=1, replica_groups=mesh['seq_0'=4,'seq_1'=4,'seq_2'=2,'tp'=4] {'seq_1'}, dimensions={0}, use_global_device_ids=true | all-gather | bytes 200 | tf_op jit(solution)/shard_map/all_gather | solution.py:44
  178.1 14.3 %all-gather.7.cloned.1.call-done = bf16[4,20,64,128]{3,2,1,0:T(8,128)(2,1)} async-done(((bf16[1,20,64,128]{3,2,1,0:T(8,128)(2,1)}), bf16[4,20,64,128]{3,2,1,0:T(8,128)(2,1)}) %all-gather.7.cloned.1.call-update) | async-done | bytes 1310736 | tf_op jit(solution)/shard_map/all_gather | solution.py:44
  192.4 2.4 fusion.60
  195.0 5.6 %reduce-window.16 = f32[20,8,128]{2,1,0:T(8,128)S(1)} reduce-window(f32[20,8,128]{2,1,0:T(8,128)S(1)} %slice.273, f32[]{:T(128)} %constant.37.clone.1), window={size=1x1x128 pad=0_0x0_0x127_0}, to_apply=%region_4.5 | reduce-window | flops 2600960 | bytes 163844 | tf_op jit(solution)/shard_map/reduce-window.2
  201.2 7.9 %all-gather.3 = bf16[4,1,20]{2,1,0:T(2,128)(2,1)S(1)} all-gather(bf16[1,1,20]{2,1,0:T(2,128)(2,1)S(1)} %get-tuple-element.164), channel_id=1, replica_groups=mesh['seq_0'=4,'seq_1'=4,'seq_2'=2,'tp'=4] {'seq_0'}, dimensions={0}, use_global_device_ids=true | all-gather | bytes 200 | tf_op jit(solution)/shard_map/all_gather | solution.py:44
  209.1 11.3 %all-gather.9.cloned.1.call-done = bf16[4,20,64,128]{3,2,1,0:T(8,128)(2,1)} async-done(((bf16[1,20,64,128]{3,2,1,0:T(8,128)(2,1)}), bf16[4,20,64,128]{3,2,1,0:T(8,128)(2,1)}) %all-gather.9.cloned.1.call-update) | async-done | bytes 1310736 | tf_op jit(solution)/shard_map/all_gather | solution.py:44
  220.4 5.8 %broadcast_multiply_fusion = f32[1024,20,64]{0,2,1:T(8,128)} fusion(f32[1024,20]{0,1:T(8,128)S(1)} %bitcast.305, bf16[4,20,64,128]{3,2,1,0:T(8,128)(2,1)} %all-gather.9.cloned.1.call-done, f32[20]{0:T(128)S(1)} %get-tuple-element.171, f32[20]{0:T(128)S(1)} %get-tuple-element.169, f32[20]{0:T(128)S(1)} %get-tuple-element.168, f32[20]{0:T(128)S(1)} %get-tuple-element.167, ...), kind=kOutput, calls=%fused_computation.66 | convolution fusion | flops 343572480 | bytes 8886282 | tf_op jit(solution)/shard_map/tn,hpn->thp/dot_general | solution.py:214
  226.2 5.9 %copy.76 = f32[1024,1280]{1,0:T(8,128)} copy(f32[1024,1280]{0,1:T(8,128)} %bitcast.294) | data formatting | bytes 10485760 | tf_op jit(solution)/shard_map/reshape | solution.py:215
  232.1 16.7 %multiply_reduce_fusion = (f32[1024]{0:T(1024)S(1)}, f32[1024]{0:T(1024)S(1)}, f32[1024,1280]{1,0:T(8,128)}) fusion(f32[1280]{0:T(1024)S(1)} %copy-done.16, bf16[1024,2560]{0,1:T(8,128)(2,1)} %bitcast.1, bf16[2560,1280]{1,0:T(8,128)(2,1)} %param.18, bf16[1024,1280]{1,0:T(8,128)(2,1)} %bitcast.293, f32[1280]{0:T(1024)S(1)} %mul.413, f32[1024,1280]{1,0:T(8,128)} %copy.76, ...), kind=kOutput, calls=%fused_computation.52 | convolution fusion | flops 6731855872 | bytes 30164992 | tf_op jit(solution)/shard_map/dot_general | solution.py:185
  249.4 4.1 %all-to-all-start.1 = ((f32[4,2,1024]{2,1,0:T(2,128)}), f32[4,2,1024]{2,1,0:T(2,128)S(1)}, u32[]{:S(2)}, u32[]{:S(2)}) async-start(f32[4,2,1024]{2,1,0:T(2,128)} %broadcast_in_dim.33), calls=%async_computation.1 | async-start | bytes 65536 | tf_op jit(solution)/shard_map/all_to_all | solution.py:61
  254.9 3.0 all-to-all-done.1
  258.0 12.7 %convolution_convert_fusion = bf16[1024,2560]{1,0:T(8,128)(2,1)} fusion(bf16[1280,2560]{1,0:T(8,128)(2,1)} %param.30, f32[1024,1280]{1,0:T(8,128)} %get-tuple-element.174, f32[]{:T(128)S(6)} %div.31, f32[1024]{0:T(1024)S(1)} %bitcast.310, f32[1280]{0:T(1024)S(1)} %copy-done.16), kind=kOutput, calls=%fused_computation.43 | convolution fusion | flops 6720061440 | bytes 17048580 | tf_op jit(solution)/shard_map/dot_general | solution.py:229
  270.7 7.9 %copy.78 = bf16[1024,2560]{0,1:T(8,128)(2,1)} copy(bf16[1024,2560]{1,0:T(8,128)(2,1)} %convolution_convert_fusion) | data formatting | bytes 10485760
  280.1 16.1 %all_to_all.16 = f32[32,1,1]{2,1,0:T(1,128)S(1)} all-to-all(f32[32,1,1]{2,1,0:T(1,128)S(1)} %broadcast_in_dim.34), channel_id=1, replica_groups=mesh['seq_0'=4,'seq_1'=4,'seq_2'=2,'tp'=4] {'seq_0','seq_1','seq_2'}, dimensions={0} | all-to-all | bytes 256 | tf_op jit(solution)/shard_map/all_to_all | solution.py:61
  298.0 37.5 %reduce-scatter.4.cloned.1.call-done = bf16[640,1024]{1,0:T(8,128)(2,1)} async-done(((bf16[2560,1024]{1,0:T(8,128)(2,1)}), bf16[640,1024]{1,0:T(8,128)(2,1)}) %reduce-scatter.4.cloned.1.call-update) | async-done | bytes 1310736
  335.5 1.7 copy.79
  (213 shorter events, 54.1 us)
Async XLA Ops:
  7.2 71.3 %copy-start = (bf16[2560,256]{1,0:T(8,128)(2,1)S(1)}, bf16[2560,256]{1,0:T(8,128)(2,1)}, u32[]{:S(2)}) copy-start(bf16[2560,256]{1,0:T(8,128)(2,1)} %param.20) | copy-start | bytes 3932164
  12.0 6.0 %copy-start.19 = (u32[128]{0:T(128)S(1)}, u32[128]{0:T(128)}, u32[]{:S(2)}) copy-start(u32[128]{0:T(128)} %constant.71) | copy-start | bytes 1540
  12.0 7.2 %copy-start.10 = (f32[4,1280]{1,0:T(4,128)S(1)}, f32[4,1280]{1,0:T(4,128)}, u32[]{:S(2)}) copy-start(f32[4,1280]{1,0:T(4,128)} %param.24) | copy-start | bytes 61444
  12.0 7.3 %copy-start.17 = (f32[20]{0:T(128)S(1)}, f32[20]{0:T(128)}, u32[]{:S(2)}) copy-start(f32[20]{0:T(128)} %param.23) | copy-start | bytes 244
  12.0 7.3 %copy-start.13 = (f32[4,256]{1,0:T(4,128)S(1)}, f32[4,256]{1,0:T(4,128)}, u32[]{:S(2)}) copy-start(f32[4,256]{1,0:T(4,128)} %param.26) | copy-start | bytes 12292
  12.0 66.5 %all-to-all-start = ((bf16[4,1024,640]{1,2,0:T(8,128)(2,1)}), bf16[4,1024,640]{1,2,0:T(8,128)(2,1)}, u32[]{:S(2)}, u32[]{:S(2)}) async-start(bf16[4,1024,640]{1,2,0:T(8,128)(2,1)} %stack.2), calls=%async_computation | async-start | bytes 10485760 | tf_op jit(solution)/shard_map/all_to_all | solution.py:16
  18.0 174.4 %all-gather.7.cloned.1.call-start = ((), (), s32[]{:S(2)}) async-start(), calls=%async_computation.4 | async-start | bytes 1638400 | tf_op jit(solution)/shard_map/all_gather | solution.py:44
  82.6 19.1 %copy-start.9 = (bf16[2560,20]{0,1:T(8,128)(2,1)S(1)}, bf16[2560,20]{0,1:T(8,128)(2,1)}, u32[]{:S(2)}) copy-start(bf16[2560,20]{0,1:T(8,128)(2,1)} %param.21) | copy-start | bytes 307204
  82.6 19.1 %copy-start.12 = (f32[20]{0:T(128)S(1)}, f32[20]{0:T(128)}, u32[]{:S(2)}) copy-start(f32[20]{0:T(128)} %param.22) | copy-start | bytes 244
  82.6 27.7 %collective-permute-start.1 = (bf16[3,256]{1,0:T(4,128)(2,1)S(1)}, bf16[3,256]{1,0:T(4,128)(2,1)S(1)}, u32[]{:S(2)}, u32[]{:S(2)}) collective-permute-start(bf16[3,256]{1,0:T(4,128)(2,1)S(1)} %slice.240), channel_id=1, source_target_pairs={{0,4},{4,8},{8,12},{12,16},{16,20},{20,24},{24,28},{28,32},{32,36}... | collective-permute-start | bytes 4616 | tf_op jit(solution)/shard_map/ppermute | solution.py:29
  99.5 10.7 %copy-start.14 = (f32[256]{0:T(256)S(1)}, f32[256]{0:T(256)}, u32[]{:S(2)}) copy-start(f32[256]{0:T(256)} %param.27) | copy-start | bytes 3076
  99.6 11.5 %copy-start.11 = (f32[1280]{0:T(1024)S(1)}, f32[1280]{0:T(1024)}, u32[]{:S(2)}) copy-start(f32[1280]{0:T(1024)} %param.25) | copy-start | bytes 15364
  99.6 11.5 %collective-permute-start = (bf16[3,1280]{1,0:T(4,128)(2,1)S(1)}, bf16[3,1280]{1,0:T(4,128)(2,1)S(1)}, u32[]{:S(2)}, u32[]{:S(2)}) collective-permute-start(bf16[3,1280]{1,0:T(4,128)(2,1)S(1)} %slice.235), channel_id=1, source_target_pairs={{0,4},{4,8},{8,12},{12,16},{16,20},{20,24},{24,28},{28,32},{32,36}... | collective-permute-start | bytes 23048 | tf_op jit(solution)/shard_map/ppermute | solution.py:29
  111.0 8.3 %copy-start.6 = (bf16[1024,256]{1,0:T(8,128)(2,1)}, bf16[1024,256]{1,0:T(8,128)(2,1)S(1)}, u32[]{:S(2)}) copy-start(bf16[1024,256]{1,0:T(8,128)(2,1)S(1)} %multiply_convert_fusion.5) | copy-start | bytes 1572868
  119.3 6.6 %copy-start.3 = (bf16[4,256,128]{2,1,0:T(8,128)(2,1)}, bf16[4,256,128]{2,1,0:T(8,128)(2,1)S(1)}, u32[]{:S(2)}) copy-start(bf16[4,256,128]{2,1,0:T(8,128)(2,1)S(1)} %get-tuple-element.260) | copy-start | bytes 786436 | tf_op jit(solution)/shard_map/while
  124.2 1.7 copy-start.2
  127.4 3.6 %copy-start.4 = (bf16[4,256,128]{2,1,0:T(8,128)(2,1)S(1)}, bf16[4,256,128]{2,1,0:T(8,128)(2,1)}, u32[]{:S(2)}) copy-start(bf16[4,256,128]{2,1,0:T(8,128)(2,1)} %copy-done.3) | copy-start | bytes 786436 | tf_op jit(solution)/shard_map/while
  131.1 6.6 %copy-start.3 = (bf16[4,256,128]{2,1,0:T(8,128)(2,1)}, bf16[4,256,128]{2,1,0:T(8,128)(2,1)S(1)}, u32[]{:S(2)}) copy-start(bf16[4,256,128]{2,1,0:T(8,128)(2,1)S(1)} %get-tuple-element.260) | copy-start | bytes 786436 | tf_op jit(solution)/shard_map/while
  139.2 3.6 %copy-start.4 = (bf16[4,256,128]{2,1,0:T(8,128)(2,1)S(1)}, bf16[4,256,128]{2,1,0:T(8,128)(2,1)}, u32[]{:S(2)}) copy-start(bf16[4,256,128]{2,1,0:T(8,128)(2,1)} %copy-done.3) | copy-start | bytes 786436 | tf_op jit(solution)/shard_map/while
  142.8 6.6 %copy-start.3 = (bf16[4,256,128]{2,1,0:T(8,128)(2,1)}, bf16[4,256,128]{2,1,0:T(8,128)(2,1)S(1)}, u32[]{:S(2)}) copy-start(bf16[4,256,128]{2,1,0:T(8,128)(2,1)S(1)} %get-tuple-element.260) | copy-start | bytes 786436 | tf_op jit(solution)/shard_map/while
  151.0 3.7 %copy-start.4 = (bf16[4,256,128]{2,1,0:T(8,128)(2,1)S(1)}, bf16[4,256,128]{2,1,0:T(8,128)(2,1)}, u32[]{:S(2)}) copy-start(bf16[4,256,128]{2,1,0:T(8,128)(2,1)} %copy-done.3) | copy-start | bytes 786436 | tf_op jit(solution)/shard_map/while
  154.7 6.6 %copy-start.3 = (bf16[4,256,128]{2,1,0:T(8,128)(2,1)}, bf16[4,256,128]{2,1,0:T(8,128)(2,1)S(1)}, u32[]{:S(2)}) copy-start(bf16[4,256,128]{2,1,0:T(8,128)(2,1)S(1)} %get-tuple-element.260) | copy-start | bytes 786436 | tf_op jit(solution)/shard_map/while
  162.8 3.6 %copy-start.4 = (bf16[4,256,128]{2,1,0:T(8,128)(2,1)S(1)}, bf16[4,256,128]{2,1,0:T(8,128)(2,1)}, u32[]{:S(2)}) copy-start(bf16[4,256,128]{2,1,0:T(8,128)(2,1)} %copy-done.3) | copy-start | bytes 786436 | tf_op jit(solution)/shard_map/while
  166.5 28.4 %copy-start.15 = (f32[20]{0:T(128)S(1)}, f32[20]{0:T(128)}, u32[]{:S(2)}) copy-start(f32[20]{0:T(128)} %param.28) | copy-start | bytes 244
  166.5 28.5 %copy-start.8 = (f32[20,1024]{1,0:T(8,128)S(1)}, f32[20,1024]{1,0:T(8,128)}, u32[]{:S(2)}) copy-start(f32[20,1024]{1,0:T(8,128)} %get-tuple-element.172) | copy-start | bytes 245764
  166.5 53.9 %copy-start.7 = (bf16[1024,256]{1,0:T(8,128)(2,1)S(1)}, bf16[1024,256]{1,0:T(8,128)(2,1)}, u32[]{:S(2)}) copy-start(bf16[1024,256]{1,0:T(8,128)(2,1)} %copy-done.6) | copy-start | bytes 1572868
  170.0 50.4 %all-gather.9.cloned.1.call-start = ((), (), s32[]{:S(2)}) async-start(), calls=%async_computation.5 | async-start | bytes 1638400 | tf_op jit(solution)/shard_map/all_gather | solution.py:44
  226.2 5.9 %copy-start.16 = (f32[1280]{0:T(1024)S(1)}, f32[1280]{0:T(1024)}, u32[]{:S(2)}) copy-start(f32[1280]{0:T(1024)} %param.29) | copy-start | bytes 15364
  232.1 21.5 %copy-start.18 = (f32[16]{0:T(128)S(1)}, f32[16]{0:T(128)}, u32[]{:S(2)}) copy-start(f32[16]{0:T(128)} %param.31) | copy-start | bytes 196
  249.4 8.4 %all-to-all-start.1 = ((f32[4,2,1024]{2,1,0:T(2,128)}), f32[4,2,1024]{2,1,0:T(2,128)S(1)}, u32[]{:S(2)}, u32[]{:S(2)}) async-start(f32[4,2,1024]{2,1,0:T(2,128)} %broadcast_in_dim.33), calls=%async_computation.1 | async-start | bytes 65536 | tf_op jit(solution)/shard_map/all_to_all | solution.py:61
  253.6 81.9 %reduce-scatter.4.cloned.1.call-start = ((), (), s32[]{:S(2)}) async-start(), calls=%async_computation.6 | async-start | bytes 6553600
  278.7 59.9 %copy-start.1 = (bf16[2560,256]{1,0:T(8,128)(2,1)S(1)}, bf16[2560,256]{1,0:T(8,128)(2,1)}, u32[]{:S(2)}) copy-start(bf16[2560,256]{1,0:T(8,128)(2,1)} %param.20) | copy-start | bytes 3932164
  (4 other events, 6.7 us)
Sparse Core Ops, SparseCore 0:
  170.1 22.2 all-gather.6
  194.9 25.4 all-gather.8
  278.8 56.6 reduce-scatter.3
